TPU v7x, 32 devices: a 4x4x1 block of a 4x4x8 slice. The times are simulated.
32 devices in a mesh: dp: 1 (over z), ep: 32 (over y, x, core).
Axes of the slice: x: 4, y: 4, z: 1, core: 2. Of those that a mesh axis runs over, the one named last changes fastest.
The devices are a block of a 4x4x8 slice.
Arguments:
- tokens: bfloat16 [49152, 768], P(('dp', 'ep'))
- w_gate: float32 [768, 128], replicated
- first_ids: int32 [49152], P(('dp', 'ep'))
- second_ids: int32 [49152], P(('dp', 'ep'))
- keep_two: int32 [49152], P(('dp', 'ep'))
- w_in: bfloat16 [128, 768, 3072], P('ep')
- w_out: bfloat16 [128, 3072, 768], P('ep')
Outputs:
- output: bfloat16 [49152, 768], P(('dp', 'ep'))
All inputs are finite; a program needn't handle non-finite values.
Results may differ from a plain program's by a relative error of at most 0.00484227.
Values are sent between devices in bfloat16 or wider.
A program may use at most 768 MiB of HBM per device.

v0:
```python
import jax
import jax.numpy as jnp
from jax import lax
from jax.sharding import PartitionSpec as P


def route_group(tokens, w_gate, first_ids, second_ids, keep_two, num_experts, capacity):
    logits = jnp.dot(tokens.astype(jnp.float32), w_gate)
    gate_probs = jax.nn.softmax(logits, axis=-1)
    expert_ids = jnp.arange(num_experts, dtype=jnp.int32)
    hot_first = (first_ids[:, None] == expert_ids[None, :]).astype(jnp.int32)
    hot_second = (second_ids[:, None] == expert_ids[None, :]).astype(jnp.int32)
    gate_one = jnp.sum(jnp.where(hot_first > 0, gate_probs, 0.0), axis=1)
    gate_two = jnp.sum(jnp.where(hot_second > 0, gate_probs, 0.0), axis=1)
    gate_sum = gate_one + gate_two
    pos_one = jnp.sum((jnp.cumsum(hot_first, axis=0) - hot_first) * hot_first, axis=1)
    first_count = jnp.sum(hot_first, axis=0)
    hot_kept = hot_second * keep_two[:, None]
    pos_two = jnp.sum((jnp.cumsum(hot_kept, axis=0) - hot_kept + first_count[None, :]) * hot_second, axis=1)
    kept_one = pos_one < capacity
    kept_two = jnp.logical_and(pos_two < capacity, keep_two > 0)
    drop_slot = num_experts * capacity
    slot_one = jnp.where(kept_one, first_ids * capacity + pos_one, drop_slot)
    slot_two = jnp.where(kept_two, second_ids * capacity + pos_two, drop_slot)
    wt_one = jnp.where(kept_one, gate_one / gate_sum, 0.0)
    wt_two = jnp.where(kept_two, gate_two / gate_sum, 0.0)
    return slot_one, slot_two, wt_one, wt_two


def dispatch_group(tokens, slot_one, slot_two, num_slots):
    seq_len = tokens.shape[0]
    token_pos = jnp.arange(seq_len, dtype=jnp.int32)
    source = jnp.full((num_slots + 1,), seq_len, dtype=jnp.int32)
    source = source.at[slot_one].set(token_pos).at[slot_two].set(token_pos)
    return jnp.take(tokens, source[:num_slots], axis=0, mode="fill", fill_value=0)


def combine_group(expert_rows, slot_one, slot_two, wt_one, wt_two):
    row_one = jnp.take(expert_rows, slot_one, axis=0, mode="fill", fill_value=0).astype(jnp.float32)
    row_two = jnp.take(expert_rows, slot_two, axis=0, mode="fill", fill_value=0).astype(jnp.float32)
    return (wt_one[:, None] * row_one + wt_two[:, None] * row_two).astype(jnp.bfloat16)


def solution(mesh):
    group_count = mesh.shape["ep"]
    token_spec = P(("dp", "ep"))

    def device_step(tokens, w_gate, first_ids, second_ids, keep_two, w_in, w_out):
        seq_len, model_dim = tokens.shape
        num_experts = w_gate.shape[1]
        local_experts = w_in.shape[0]
        capacity = max(2, (2 * seq_len + num_experts - 1) // num_experts)
        slot_one, slot_two, wt_one, wt_two = route_group(tokens, w_gate, first_ids, second_ids, keep_two, num_experts, capacity)
        buffer = dispatch_group(tokens, slot_one, slot_two, num_experts * capacity)
        buffer = buffer.reshape(group_count, local_experts, capacity, model_dim)
        received = lax.all_to_all(buffer, "ep", 0, 0, tiled=True)
        hidden = jnp.maximum(jnp.einsum("pecd,edf->pecf", received, w_in, preferred_element_type=jnp.float32), 0.0).astype(jnp.bfloat16)
        expert_out = jnp.einsum("pecf,efd->pecd", hidden, w_out, preferred_element_type=jnp.float32).astype(jnp.bfloat16)
        returned = lax.all_to_all(expert_out, "ep", 0, 0, tiled=True)
        expert_rows = returned.reshape(num_experts * capacity, model_dim)
        return combine_group(expert_rows, slot_one, slot_two, wt_one, wt_two)

    return jax.shard_map(
        device_step,
        mesh=mesh,
        in_specs=(P(("dp", "ep"), None), P(), token_spec, token_spec, token_spec, P("ep"), P("ep")),
        out_specs=P(("dp", "ep"), None),
        check_vma=False,
    )
```

profile of v0, /device:TPU:103, one launch (start us, length us, event | category | flops | bytes accessed | tf_op | source)
XLA Modules:
  0.0 253.7 jit_solution(16419560472254081089)
XLA Ops:
  0.0 0.0 copy-start
  0.0 1.0 copy.37
  1.0 0.3 fusion.14
  1.3 0.1 broadcast_add_fusion.1
  1.4 0.3 copy.38
  1.7 1.1 copy.39
  2.8 2.0 convert_reduce_fusion
  4.8 0.1 copy.40
  4.9 0.8 copy.41
  5.7 0.6 fusion.12
  6.4 0.1 broadcast_add_fusion
  6.5 0.3 copy.42
  6.7 1.1 copy.43
  7.9 1.4 fusion.20
  9.3 0.7 compare_and_fusion.1
  10.0 6.2 %scatter_custom_fusion = s32[3073]{0:T(1024)S(1)} fusion(s32[1536]{0:T(1024)S(1)} %compare_select_fusion.2, s32[1536]{0:T(1024)S(1)} %iota.17, s32[]{:T(128)} %constant.27.clone.1), kind=kCustom, calls=%fused_computation.63 | custom fusion | bytes 12296 | tf_op jit(solution)/shard_map/scatter | solution.py:34
  16.2 6.2 %scatter_fusion = s32[3073]{0:T(1024)S(1)} fusion(s32[3073]{0:T(1024)S(1)} %scatter_custom_fusion, s32[1536]{0:T(1024)S(1)} %compare_select_fusion.5, s32[1536]{0:T(1024)S(1)} %iota.18), kind=kCustom, calls=%fused_computation.4 | custom fusion | bytes 24576 | tf_op jit(solution)/shard_map/scatter | solution.py:34
  22.5 0.1 slice.22
  22.7 13.5 %gather_fusion = bf16[3072,768]{1,0:T(8,128)(2,1)} fusion(bf16[1536,768]{1,0:T(8,128)(2,1)S(1)} %copy-done, s32[3072]{0:T(1024)S(1)} %get-tuple-element.18), kind=kCustom, calls=%fused_computation.2 | custom fusion | bytes 9449472 | tf_op jit(solution)/shard_map/jit(_take)/gather | solution.py:35
  36.2 2.7 %broadcast_select_fusion = bf16[32,4,24,768]{3,2,1,0:T(8,128)(2,1)S(1)} fusion(bf16[32,4,24,768]{3,2,1,0:T(8,128)(2,1)} %bitcast.44, pred[32,4,24]{2,1,0:T(4,128)(4,1)S(1)} %compare_and_fusion), kind=kLoop, calls=%fused_computation.15 | loop fusion | flops 2359296 | bytes 9440256 | tf_op jit(solution)/shard_map/jit(_take)/select_n | solution.py:35
  38.9 66.9 %all_to_all.10 = bf16[32,4,24,768]{3,2,1,0:T(8,128)(2,1)} all-to-all(bf16[32,4,24,768]{3,2,1,0:T(8,128)(2,1)S(1)} %broadcast_select_fusion), channel_id=1, replica_groups=mesh['dp'=1,'ep'=32] {'ep'}, dimensions={0} | all-to-all | bytes 9437184 | tf_op jit(solution)/shard_map/all_to_all | solution.py:56
  105.8 24.7 %fusion.4 = bf16[4,32,24,3072]{3,2,1,0:T(8,128)(2,1)} fusion(bf16[4,768,3072]{2,1,0:T(8,128)(2,1)} %param.14, bf16[32,4,24,768]{3,2,1,0:T(8,128)(2,1)} %all_to_all.10), kind=kOutput, calls=%fused_computation.9 | convolution fusion | flops 14495514624 | bytes 42467328 | tf_op jit(solution)/shard_map/pecd,edf->pecf/dot_general | solution.py:57
  130.5 24.5 %convert_bitcast_fusion = bf16[32,4,24,768]{3,2,0,1:T(8,128)(2,1)} fusion(bf16[4,3072,768]{2,1,0:T(8,128)(2,1)} %param.15, bf16[4,32,24,3072]{3,2,1,0:T(8,128)(2,1)} %fusion.4), kind=kOutput, calls=%fused_computation.14 | convolution fusion | flops 14526185472 | bytes 42467328 | tf_op jit(solution)/shard_map/pecf,efd->pecd/dot_general | solution.py:58
  155.0 5.1 %copy.45 = bf16[32,4,24,768]{3,2,1,0:T(8,128)(2,1)} copy(bf16[32,4,24,768]{3,2,0,1:T(8,128)(2,1)} %convert_bitcast_fusion) | data formatting | bytes 9437184 | tf_op jit(solution)/shard_map/convert_element_type | solution.py:58
  160.2 6.1 %all-to-all-start.1 = ((bf16[32,4,24,768]{3,2,1,0:T(8,128)(2,1)}), bf16[32,4,24,768]{3,2,1,0:T(8,128)(2,1)}, u32[]{:S(2)}, u32[]{:S(2)}) async-start(bf16[32,4,24,768]{3,2,1,0:T(8,128)(2,1)} %copy.45), calls=%async_computation.1 | async-start | bytes 9437184 | tf_op jit(solution)/shard_map/all_to_all | solution.py:59
  166.3 0.9 fusion.35
  167.3 0.1 fusion.22
  167.4 0.3 select_reduce_fusion.1
  167.7 61.5 %all-to-all-done.1 = bf16[32,4,24,768]{3,2,1,0:T(8,128)(2,1)} async-done(((bf16[32,4,24,768]{3,2,1,0:T(8,128)(2,1)}), bf16[32,4,24,768]{3,2,1,0:T(8,128)(2,1)}, u32[]{:S(2)}, u32[]{:S(2)}) %all-to-all-start.1) | async-done | bytes 4718624 | tf_op jit(solution)/shard_map/all_to_all | solution.py:59
  229.2 9.6 %gather_fusion.2 = bf16[1536,768]{1,0:T(8,128)(2,1)} fusion(bf16[3072,768]{1,0:T(8,128)(2,1)} %bitcast.16, s32[2048]{0:T(1024)S(1)} %pad_clamp_fusion), kind=kCustom, calls=%fused_computation.1.clone | custom fusion | bytes 4724736 | tf_op jit(solution)/shard_map/jit(_take)/gather | solution.py:40
  238.9 9.6 %gather_fusion.1 = bf16[1536,768]{1,0:T(8,128)(2,1)} fusion(bf16[3072,768]{1,0:T(8,128)(2,1)} %bitcast.16, s32[2048]{0:T(1024)S(1)} %pad_clamp_fusion.1), kind=kCustom, calls=%fused_computation.clone | custom fusion | bytes 4724736 | tf_op jit(solution)/shard_map/jit(_take)/gather | solution.py:39
  248.5 5.2 %add_convert_fusion = bf16[1536,768]{1,0:T(8,128)(2,1)} fusion(bf16[1536,768]{1,0:T(8,128)(2,1)} %gather_fusion.2, bf16[1536,768]{1,0:T(8,128)(2,1)} %gather_fusion.1, f32[1536]{0:T(1024)S(1)} %get-tuple-element.16, f32[1536]{0:T(1024)S(1)} %get-tuple-element.15, pred[1536]{0:T(1024)(128)(4,1)S(1)} %get-tuple-element.12, ...), kind=kLoop, calls=%fused_computation.13 | loop fusion | flops 9437184 | bytes 7093248 | tf_op jit(solution)/shard_map/convert_element_type | solution.py:41
  (25 shorter events, 0.2 us)
Async XLA Ops:
  0.0 22.6 %copy-start = (bf16[1536,768]{1,0:T(8,128)(2,1)S(1)}, bf16[1536,768]{1,0:T(8,128)(2,1)}, u32[]{:S(2)}) copy-start(bf16[1536,768]{1,0:T(8,128)(2,1)} %param.9) | copy-start | bytes 7077892
  0.0 2.8 %copy-start.2 = (s32[1536]{0:T(1024)S(1)}, s32[1536]{0:T(1024)}, u32[]{:S(2)}) copy-start(s32[1536]{0:T(1024)} %param.11) | copy-start | bytes 18436
  0.0 4.8 %copy-start.3 = (s32[1536]{0:T(1024)S(1)}, s32[1536]{0:T(1024)}, u32[]{:S(2)}) copy-start(s32[1536]{0:T(1024)} %param.12) | copy-start | bytes 18436
  6.3 1.6 copy-start.5
  6.3 3.7 %copy-start.4 = (s32[1536]{0:T(1024)S(1)}, s32[1536]{0:T(1024)}, u32[]{:S(2)}) copy-start(s32[1536]{0:T(1024)} %get-tuple-element.9) | copy-start | bytes 18436
  160.2 6.2 %copy-start.1 = (f32[768,128]{1,0:T(8,128)S(1)}, f32[768,128]{1,0:T(8,128)}, u32[]{:S(2)}) copy-start(f32[768,128]{1,0:T(8,128)} %param.10) | copy-start | bytes 1179652
  160.2 69.1 %all-to-all-start.1 = ((bf16[32,4,24,768]{3,2,1,0:T(8,128)(2,1)}), bf16[32,4,24,768]{3,2,1,0:T(8,128)(2,1)}, u32[]{:S(2)}, u32[]{:S(2)}) async-start(bf16[32,4,24,768]{3,2,1,0:T(8,128)(2,1)} %copy.45), calls=%async_computation.1 | async-start | bytes 9437184 | tf_op jit(solution)/shard_map/all_to_all | solution.py:59
where the time goes:
time: 254 us
  blocking collectives  66.9 us (26%)
  waiting for transfers between devices  61.5 us (24%)
  local copies, waits for them, and re-layouts  55.2 us (22%)
  matrix products  50.2 us (20%)
  other arithmetic  13.6 us (5%)
  starting transfers between devices  6.13 us (2%)
    all_to_all x1, blocking collectives, device_step(): received = lax.all_to_all(buffer, 'ep', 0, 0, tiled=True)  66.9 us
    all_to_all x1, waiting for transfers between devices, device_step(): returned = lax.all_to_all(expert_out, 'ep', 0, 0, tiled=True)  61.5 us
    dot_general x1, matrix products, device_step(): jnp.einsum('pecd,edf->pecf', received, w_in, preferred_element_type=jnp.f...  24.7 us
    dot_general x1, matrix products, device_step(): jnp.einsum('pecf,efd->pecd', hidden, w_out, preferred_element_type=jnp.fl...  24.5 us
    gather x1, local copies, waits for them, and re-layouts, dispatch_group(): jnp.take(tokens, source[:num_slots], axis=0, mode='fill', fill_value=0)  13.5 us
    scatter x2, local copies, waits for them, and re-layouts, dispatch_group(): source = source.at[slot_one].set(token_pos).at[slot_two].set(token_pos)  12.4 us
    gather x1, local copies, waits for them, and re-layouts, combine_group(): jnp.take(expert_rows, slot_one, axis=0, mode='fill', fill_value=0)  9.64 us
    gather x1, local copies, waits for them, and re-layouts, combine_group(): jnp.take(expert_rows, slot_two, axis=0, mode='fill', fill_value=0)  9.63 us
  transfers between devices with their start and end apart: 1, of which 1 were waited for; matrix products, arithmetic and copies ran while one was open for 1% of the time, Pallas kernels for 0%

commit v1 on v0

v1 whole, which is shorter than its diff:
```python
import functools
import jax
import jax.numpy as jnp
from jax import lax
from jax.experimental import pallas as pl
from jax.experimental.pallas import tpu as pltpu
from jax.sharding import PartitionSpec as P

F32, BF16, I32 = jnp.float32, jnp.bfloat16, jnp.int32
VMEM_LIMIT = 67_000_000


def iota(shape, axis):
    return lax.broadcasted_iota(I32, shape, axis)


def slots_by_row(first, second, keep, num_experts, local_experts, capacity):
    seq_len = first.shape[1]
    block = 256
    expert = iota((num_experts, seq_len), 0)
    hot_first = (expert == first).astype(F32)
    hot_second = (expert == second).astype(F32)
    hot_kept = hot_second * keep.astype(F32)
    hot = jnp.concatenate([hot_first, hot_kept], axis=0)
    before = (iota((block, block), 0) < iota((block, block), 1)).astype(BF16)
    count = jnp.zeros((2 * num_experts, 1), F32)
    earlier = []
    for start in range(0, seq_len, block):
        part = hot[:, start : start + block]
        earlier.append(jnp.dot(part.astype(BF16), before, preferred_element_type=F32) + count)
        count = count + jnp.sum(part, axis=1, keepdims=True)
    earlier = jnp.concatenate(earlier, axis=1)
    pos_one = jnp.sum(earlier[:num_experts] * hot_first, axis=0, keepdims=True)
    pos_two = jnp.sum((earlier[num_experts:] + count[:num_experts]) * hot_second, axis=0, keepdims=True)
    pos_one, pos_two = pos_one.astype(I32), pos_two.astype(I32)
    span = num_experts // local_experts * capacity

    def slot(ids, pos, kept):
        return jnp.where(kept, (ids % local_experts) * span + (ids // local_experts) * capacity + pos, -1)

    kept_two = jnp.logical_and(pos_two < capacity, keep > 0)
    return slot(first, pos_one, pos_one < capacity), slot(second, pos_two, kept_two)


def columns_of(rows, seq_len):
    sublane = iota((128, seq_len), 0)
    stacked = jnp.zeros((128, seq_len), F32)
    for i, row in enumerate(rows):
        stacked = jnp.where(sublane == i, row.astype(F32), stacked)
    return stacked.T


def gates_of(tokens, w_gate, first, second):
    num_experts = w_gate.shape[1]
    high = w_gate.astype(BF16)
    rest = w_gate - high.astype(F32)
    mid = rest.astype(BF16)
    low = (rest - mid.astype(F32)).astype(BF16)
    logits = (
        jnp.dot(tokens, low, preferred_element_type=F32)
        + jnp.dot(tokens, mid, preferred_element_type=F32)
        + jnp.dot(tokens, high, preferred_element_type=F32)
    )
    odds = jnp.exp(logits - jnp.max(logits, axis=1, keepdims=True))
    probs = odds / jnp.sum(odds, axis=1, keepdims=True)
    expert = iota((tokens.shape[0], num_experts), 1).astype(F32)
    gate_one = jnp.sum(jnp.where(expert == first, probs, 0.0), axis=1, keepdims=True)
    gate_two = jnp.sum(jnp.where(expert == second, probs, 0.0), axis=1, keepdims=True)
    total = gate_one + gate_two
    return gate_one / total, gate_two / total


def route_kernel(local_experts, capacity, tokens_ref, w_gate_ref, first_ref, second_ref, keep_ref, buffer_ref, plan_ref):
    seq_len = tokens_ref.shape[0]
    num_experts = w_gate_ref.shape[1]
    first, second = first_ref[...], second_ref[...]
    slot_one, slot_two = slots_by_row(first, second, keep_ref[...], num_experts, local_experts, capacity)
    span = buffer_ref.shape[1]
    rows = 256

    @pl.loop(0, local_experts * span // rows)
    def _(step):
        local = step // (span // rows)
        part = step % (span // rows)
        row = iota((rows, seq_len), 0) + step * rows
        pick = jnp.logical_or(row == slot_one, row == slot_two)
        pick = jnp.where(pick, 1.0, 0.0).astype(BF16)
        picked = jnp.dot(pick, tokens_ref[...], preferred_element_type=F32)
        buffer_ref[local, pl.ds(part * rows, rows), :] = picked.astype(BF16)

    columns = columns_of((first, second, slot_one, slot_two), seq_len)
    gate_one, gate_two = gates_of(tokens_ref[...], w_gate_ref[...], columns[:, 0:1], columns[:, 1:2])
    lane = iota((seq_len, 128), 1)
    plan_ref[...] = jnp.where(
        lane == 0, columns[:, 2:3], jnp.where(lane == 1, columns[:, 3:4], jnp.where(lane == 2, gate_one, gate_two))
    )


def exchange_kernel(
    n, local_experts, buffer_ref, w_in_ref, w_out_ref, returned_ref,
    recv, w_in, w_out, hidden, send_sem, recv_sem, back_sem, w_sem,
):
    me = lax.axis_index("ep")
    model_dim, ff_dim = w_in.shape[1:]
    capacity = buffer_ref.shape[2]
    span = n * capacity

    def fetch(e):
        return (
            pltpu.make_async_copy(w_in_ref.at[e], w_in.at[e % 2], w_sem.at[0, e % 2]),
            pltpu.make_async_copy(w_out_ref.at[e], w_out.at[e % 2], w_sem.at[1, e % 2]),
        )

    barrier = pltpu.get_barrier_semaphore()

    @pl.loop(1, n)
    def _(k):
        pl.semaphore_signal(barrier, inc=1, device_id={"ep": lax.rem(me + k, n)}, device_id_type=pl.DeviceIdType.MESH)

    for copy in fetch(0):
        copy.start()
    pl.semaphore_wait(barrier, n - 1)

    def send(source, target, sem, e):
        @pl.loop(1, n)
        def _(k):
            peer = lax.rem(me + k, n)
            pltpu.make_async_remote_copy(
                src_ref=source.at[e, peer],
                dst_ref=target.at[e, me],
                send_sem=send_sem,
                recv_sem=sem.at[e],
                device_id={"ep": peer},
                device_id_type=pl.DeviceIdType.MESH,
            ).start()

    for e in range(local_experts):
        send(buffer_ref, recv, recv_sem, e)
        recv[e, me] = buffer_ref[e, me]

    for e in range(local_experts):
        if e + 1 < local_experts:
            for copy in fetch(e + 1):
                copy.start()
        arrived = recv.at[e, pl.ds(0, n - 1)]
        pltpu.make_async_copy(arrived, arrived, recv_sem.at[e]).wait()
        into, out = fetch(e)
        into.wait()
        wide = 512

        @pl.loop(0, ff_dim // wide)
        def _(j):
            at = pl.ds(pl.multiple_of(j * wide, wide), wide)
            up = jnp.dot(recv[e].reshape(span, model_dim), w_in[e % 2, :, at], preferred_element_type=F32)
            hidden[:, at] = jnp.maximum(up, 0.0).astype(BF16)

        out.wait()
        tall = 256

        @pl.loop(0, span // tall)
        def _(i):
            at = pl.ds(pl.multiple_of(i * tall, tall), tall)
            down = jnp.dot(hidden[at, :], w_out[e % 2], preferred_element_type=F32)
            hidden[at, 0:model_dim] = down.astype(BF16)

        recv[e] = hidden[:, 0:model_dim].reshape(n, capacity, model_dim)
        send(recv, returned_ref, back_sem, e)
        own = pltpu.make_async_copy(recv.at[e, me], returned_ref.at[e, me], w_sem.at[2, 0])
        own.start()
        own.wait()

    for e in range(local_experts):
        arrived = returned_ref.at[e, pl.ds(0, n - 1)]
        pltpu.make_async_copy(arrived, arrived, back_sem.at[e]).wait()
    sent = recv.at[:, pl.ds(0, n - 1)]
    pltpu.make_async_copy(sent, sent, send_sem).wait()
    pltpu.make_async_copy(sent, sent, send_sem).wait()


def combine_kernel(plan_ref, rows_ref, out_ref):
    seq_len = out_ref.shape[0]
    slots = rows_ref.shape[0]
    tall = 256

    @pl.loop(0, seq_len // tall)
    def _(i):
        at = pl.ds(pl.multiple_of(i * tall, tall), tall)
        plan = plan_ref[at, :]
        slot = iota((tall, slots), 1).astype(F32)
        pick = jnp.where(slot == plan[:, 0:1], 1.0, 0.0).astype(BF16)
        total = plan[:, 2:3] * jnp.dot(pick, rows_ref[...], preferred_element_type=F32)
        pick = jnp.where(slot == plan[:, 1:2], 1.0, 0.0).astype(BF16)
        total = total + plan[:, 3:4] * jnp.dot(pick, rows_ref[...], preferred_element_type=F32)
        out_ref[at, :] = total.astype(BF16)


def solution(mesh):
    n = mesh.shape["ep"]
    token_spec = P(("dp", "ep"))
    vmem = pl.BlockSpec(memory_space=pltpu.VMEM)
    hbm = pl.BlockSpec(memory_space=pl.ANY)

    def device_step(tokens, w_gate, first_ids, second_ids, keep_two, w_in, w_out):
        seq_len, model_dim = tokens.shape
        num_experts = w_gate.shape[1]
        local_experts, _, ff_dim = w_in.shape
        capacity = max(2, (2 * seq_len + num_experts - 1) // num_experts)
        span = n * capacity
        buffer, plan = pl.pallas_call(
            functools.partial(route_kernel, local_experts, capacity),
            out_shape=(
                jax.ShapeDtypeStruct((local_experts, span, model_dim), BF16),
                jax.ShapeDtypeStruct((seq_len, 128), F32),
            ),
            in_specs=[vmem] * 5,
            out_specs=(vmem, vmem),
            compiler_params=pltpu.CompilerParams(vmem_limit_bytes=VMEM_LIMIT),
        )(tokens, w_gate, first_ids[None], second_ids[None], keep_two[None])
        slab = (local_experts, n, capacity, model_dim)
        returned = pl.pallas_call(
            functools.partial(exchange_kernel, n, local_experts),
            out_shape=jax.ShapeDtypeStruct(slab, BF16),
            in_specs=[vmem, hbm, hbm],
            out_specs=hbm,
            scratch_shapes=[
                pltpu.VMEM(slab, BF16),
                pltpu.VMEM((2, model_dim, ff_dim), BF16),
                pltpu.VMEM((2, ff_dim, model_dim), BF16),
                pltpu.VMEM((span, ff_dim), BF16),
                pltpu.SemaphoreType.DMA,
                pltpu.SemaphoreType.DMA((local_experts,)),
                pltpu.SemaphoreType.DMA((local_experts,)),
                pltpu.SemaphoreType.DMA((3, 2)),
            ],
            compiler_params=pltpu.CompilerParams(collective_id=0, has_side_effects=True, vmem_limit_bytes=VMEM_LIMIT),
        )(buffer.reshape(slab), w_in, w_out)
        return pl.pallas_call(
            combine_kernel,
            out_shape=jax.ShapeDtypeStruct((seq_len, model_dim), BF16),
            in_specs=[vmem, vmem],
            out_specs=vmem,
            compiler_params=pltpu.CompilerParams(vmem_limit_bytes=VMEM_LIMIT),
        )(plan, returned.reshape(local_experts * span, model_dim))

    return jax.shard_map(
        device_step,
        mesh=mesh,
        in_specs=(P(("dp", "ep"), None), P(), token_spec, token_spec, token_spec, P("ep"), P("ep")),
        out_specs=P(("dp", "ep"), None),
        check_vma=False,
    )
```

time: 254 us -> 166 us (0.65)
  the two profiles are of different devices: /device:TPU:103 before, /device:TPU:97 now
where the time goes in v1:
time: 166 us; the launch traced here: 165 us
  Pallas kernels  161 us (97%)
  local copies, waits for them, and re-layouts  3.88 us (2%)
    pallas_call x1, Pallas kernels, device_step(): pl.pallas_call(functools.partial(exchange_kernel, n, local_experts), out_...  125 us
    pallas_call x1, Pallas kernels, device_step(): pl.pallas_call(combine_kernel, out_shape=jax.ShapeDtypeStruct((seq_len, m...  19.9 us
    pallas_call x1, Pallas kernels, device_step(): pl.pallas_call(functools.partial(route_kernel, local_experts, capacity),...  16.3 us

profile of v1, /device:TPU:97, one launch (start us, length us, event | category | flops | bytes accessed | tf_op | source)
XLA Modules:
  0.0 165.2 jit_solution(14087495128896100111)
XLA Ops:
  0.0 1.3 broadcast_in_dim.9.first_ref
  1.3 1.3 broadcast_in_dim.10.second_ref
  2.6 1.3 broadcast_in_dim.11.keep_ref
  3.9 16.3 %shard_map.73 = (bf16[4,768,768]{2,1,0:T(8,128)(2,1)}, f32[1536,128]{1,0:T(8,128)}) custom-call(bf16[1536,768]{1,0:T(8,128)(2,1)} %tokens_ref.1, f32[768,128]{1,0:T(8,128)} %w_gate_ref.1, s32[1,1536]{1,0:T(1,128)} %broadcast_in_dim.9.first_ref, s32[1,1536]{1,0:T(1,128)} %broadcast_in_dim.10.second_ref, s32[1,1536]{1,0:T(1,128)} %broadcast_in_dim.11.keep_ref), custom_call_target="tpu_custom_call" | custom-call | tf_op jit(solution)/shard_map/pallas_call | solution.py:209
  20.2 125.1 %shard_map.74 = bf16[4,32,24,768]{3,2,1,0:T(8,128)(2,1)} custom-call(bf16[4,32,24,768]{3,2,1,0:T(8,128)(2,1)} %bitcast.3, bf16[4,768,3072]{2,1,0:T(8,128)(2,1)} %w_in_ref.1, bf16[4,3072,768]{2,1,0:T(8,128)(2,1)} %w_out_ref.1), custom_call_target="tpu_custom_call" | custom-call | tf_op jit(solution)/shard_map/pallas_call | solution.py:220
  145.3 19.9 %shard_map.75 = bf16[1536,768]{1,0:T(8,128)(2,1)} custom-call(f32[1536,128]{1,0:T(8,128)} %get-tuple-element.7.plan_ref, bf16[3072,768]{1,0:T(8,128)(2,1)} %bitcast.2), custom_call_target="tpu_custom_call" | custom-call | tf_op jit(solution)/shard_map/pallas_call | solution.py:237

commit v2 on v1

v2 whole, which is shorter than its diff:
```python
import functools
import math
import jax
import jax.numpy as jnp
from jax import lax
from jax.experimental import pallas as pl
from jax.experimental.pallas import tpu as pltpu
from jax.sharding import PartitionSpec as P

F32, BF16, I32 = jnp.float32, jnp.bfloat16, jnp.int32
VMEM_LIMIT = 67_000_000


def iota(shape, axis):
    return lax.broadcasted_iota(I32, shape, axis)


def peer_offsets(n):
    side = math.isqrt(n // 2)
    cells = [(dy, dx) for dy in range(side) for dx in range(side) if dy or dx]
    near = {step: min(step, side - step) for step in range(side)}
    cells.sort(key=lambda cell: (-near[cell[0]] - near[cell[1]], cell))
    order = [(0, 0, 0), (0, 0, 1)] + [(dy, dx, core) for core in range(2) for dy, dx in cells]
    return side, order


def row_of(ref):
    return jnp.concatenate([ref[i : i + 1, :] for i in range(ref.shape[0])], axis=1)


def slots_by_row(first, second, keep, num_experts, local_experts, capacity, place):
    seq_len = first.shape[1]
    block = 256
    expert = iota((num_experts, seq_len), 0)
    hot_first = (expert == first).astype(F32)
    hot_second = (expert == second).astype(F32)
    hot_kept = hot_second * keep.astype(F32)
    hot = jnp.concatenate([hot_first, hot_kept], axis=0)
    before = (iota((block, block), 0) < iota((block, block), 1)).astype(BF16)
    count = jnp.zeros((2 * num_experts, 1), F32)
    earlier = []
    for start in range(0, seq_len, block):
        part = hot[:, start : start + block]
        earlier.append(jnp.dot(part.astype(BF16), before, preferred_element_type=F32) + count)
        count = count + jnp.sum(part, axis=1, keepdims=True)
    earlier = jnp.concatenate(earlier, axis=1)
    pos_one = jnp.sum(earlier[:num_experts] * hot_first, axis=0, keepdims=True)
    pos_two = jnp.sum((earlier[num_experts:] + count[:num_experts]) * hot_second, axis=0, keepdims=True)
    pos_one, pos_two = pos_one.astype(I32), pos_two.astype(I32)
    span = num_experts // local_experts * capacity

    def slot(ids, pos, kept):
        return jnp.where(kept, (ids % local_experts) * span + place(ids // local_experts) * capacity + pos, -1)

    kept_two = jnp.logical_and(pos_two < capacity, keep > 0)
    return slot(first, pos_one, pos_one < capacity), slot(second, pos_two, kept_two)


def columns_of(rows, seq_len):
    sublane = iota((128, seq_len), 0)
    stacked = jnp.zeros((128, seq_len), F32)
    for i, row in enumerate(rows):
        stacked = jnp.where(sublane == i, row.astype(F32), stacked)
    return stacked.T


def gates_of(tokens, w_gate, first, second):
    num_experts = w_gate.shape[1]
    high = w_gate.astype(BF16)
    rest = w_gate - high.astype(F32)
    mid = rest.astype(BF16)
    low = (rest - mid.astype(F32)).astype(BF16)
    logits = (
        jnp.dot(tokens, low, preferred_element_type=F32)
        + jnp.dot(tokens, mid, preferred_element_type=F32)
        + jnp.dot(tokens, high, preferred_element_type=F32)
    )
    odds = jnp.exp(logits - jnp.max(logits, axis=1, keepdims=True))
    probs = odds / jnp.sum(odds, axis=1, keepdims=True)
    expert = iota((tokens.shape[0], num_experts), 1).astype(F32)
    gate_one = jnp.sum(jnp.where(expert == first, probs, 0.0), axis=1, keepdims=True)
    gate_two = jnp.sum(jnp.where(expert == second, probs, 0.0), axis=1, keepdims=True)
    total = gate_one + gate_two
    return gate_one / total, gate_two / total


def layer_kernel(
    n, local_experts, capacity, tokens_hbm, w_gate_ref, first_ref, second_ref, keep_ref, w_in_ref, w_out_ref, out_ref,
    tokens, buffer, recv, returned, w_in, w_out, hidden, total, plan, send_sem, recv_sem, back_sem, w_sem, tok_sem,
):
    me = lax.axis_index("ep")
    seq_len, model_dim = tokens.shape
    num_experts = w_gate_ref.shape[1]
    ff_dim = w_in.shape[2]
    span = n * capacity
    side, order = peer_offsets(n)
    my_core, my_x, my_y = me % 2, me // 2 % side, me // (2 * side)
    group = 8
    rows = group * capacity

    def fetch(e):
        return (
            pltpu.make_async_copy(w_in_ref.at[e], w_in.at[e % 2], w_sem.at[0, e % 2]),
            pltpu.make_async_copy(w_out_ref.at[e], w_out.at[e % 2], w_sem.at[1, e % 2]),
        )

    load = pltpu.make_async_copy(tokens_hbm, tokens, tok_sem)
    load.start()
    barrier = pltpu.get_barrier_semaphore()

    @pl.loop(1, n)
    def _(k):
        pl.semaphore_signal(barrier, inc=1, device_id={"ep": lax.rem(me + k, n)}, device_id_type=pl.DeviceIdType.MESH)

    for e in range(min(2, local_experts)):
        for copy in fetch(e):
            copy.start()

    def place(device):
        core = (device - my_core) % 2
        x = (device // 2 - my_x + side) % side
        y = (device // (2 * side) - my_y + side) % side
        flat = (y * side + x) * 2 + core
        at = jnp.zeros_like(device)
        for i, (dy, dx, dc) in enumerate(order):
            at = jnp.where(flat == (dy * side + dx) * 2 + dc, i, at)
        return at

    first, second, keep = row_of(first_ref), row_of(second_ref), row_of(keep_ref)
    slot_one, slot_two = slots_by_row(first, second, keep, num_experts, local_experts, capacity, place)

    def send(source, target, sem, e, part):
        for i in range(part * group, (part + 1) * group):
            if i == 0:
                continue
            dy, dx, dc = order[i]
            back = order.index(((side - dy) % side, (side - dx) % side, dc))
            peer = ((my_y + dy) % side * side + (my_x + dx) % side) * 2 + (my_core + dc) % 2
            pltpu.make_async_remote_copy(
                src_ref=source.at[e, i],
                dst_ref=target.at[e, back],
                send_sem=send_sem,
                recv_sem=sem.at[e],
                device_id={"ep": peer},
                device_id_type=pl.DeviceIdType.MESH,
            ).start()

    def build(e, part):
        row = iota((rows, seq_len), 0) + (e * span + part * rows)
        pick = jnp.logical_or(row == slot_one, row == slot_two)
        pick = jnp.where(pick, 1.0, 0.0).astype(BF16)
        picked = jnp.dot(pick, tokens[...], preferred_element_type=F32).astype(BF16)
        buffer[e, part * group : (part + 1) * group] = picked.reshape(group, capacity, model_dim)

    parts = n // group
    load.wait()
    pl.semaphore_wait(barrier, n - 1)

    @pl.loop(0, local_experts)
    def _(e):
        for part in range(parts):
            build(e, part)
            if part:
                send(buffer, recv, recv_sem, e, part - 1)
        recv[e, 0] = buffer[e, 0]
        send(buffer, recv, recv_sem, e, parts - 1)

    columns = columns_of((first, second, slot_one, slot_two), seq_len)
    gate_one, gate_two = gates_of(tokens[...], w_gate_ref[...], columns[:, 0:1], columns[:, 1:2])
    lane = iota((seq_len, 128), 1)
    plan[...] = jnp.where(
        lane == 0, columns[:, 2:3], jnp.where(lane == 1, columns[:, 3:4], jnp.where(lane == 2, gate_one, gate_two))
    )

    for e in range(local_experts):
        arrived = recv.at[e, pl.ds(1, n - 1)]
        pltpu.make_async_copy(arrived, arrived, recv_sem.at[e]).wait()
        into, out = fetch(e)
        into.wait()
        wide = 512

        @pl.loop(0, ff_dim // wide)
        def _(j):
            at = pl.ds(pl.multiple_of(j * wide, wide), wide)
            up = jnp.dot(recv[e].reshape(span, model_dim), w_in[e % 2, :, at], preferred_element_type=F32)
            hidden[:, at] = jnp.maximum(up, 0.0).astype(BF16)

        out.wait()
        for part in range(parts):
            down = jnp.dot(hidden[part * rows : (part + 1) * rows, :], w_out[e % 2], preferred_element_type=F32)
            recv[e, part * group : (part + 1) * group] = down.astype(BF16).reshape(group, capacity, model_dim)
            if part:
                send(recv, returned, back_sem, e, part - 1)
        returned[e, 0] = recv[e, 0]
        send(recv, returned, back_sem, e, parts - 1)
        if e + 2 < local_experts:
            for copy in fetch(e + 2):
                copy.start()

    tall = 256
    for e in range(local_experts):
        arrived = returned.at[e, pl.ds(1, n - 1)]
        pltpu.make_async_copy(arrived, arrived, back_sem.at[e]).wait()

        @pl.loop(0, seq_len // tall)
        def _(i):
            at = pl.ds(pl.multiple_of(i * tall, tall), tall)
            part = plan[at, :]
            slot = (iota((tall, span), 1) + e * span).astype(F32)
            pick = jnp.concatenate(
                [jnp.where(slot == part[:, c : c + 1], 1.0, 0.0).astype(BF16) for c in range(2)], axis=0
            )
            picked = jnp.dot(pick, returned[e].reshape(span, model_dim), preferred_element_type=F32)
            added = part[:, 2:3] * picked[:tall] + part[:, 3:4] * picked[tall:]
            if e:
                added = total[at, :] + added
            if e + 1 < local_experts:
                total[at, :] = added
            else:
                out_ref[at, :] = added.astype(BF16)

    sent = recv.at[:, pl.ds(1, n - 1)]
    pltpu.make_async_copy(sent, sent, send_sem).wait()
    pltpu.make_async_copy(sent, sent, send_sem).wait()


def solution(mesh):
    n = mesh.shape["ep"]
    token_spec = P(("dp", "ep"))
    vmem = pl.BlockSpec(memory_space=pltpu.VMEM)
    hbm = pl.BlockSpec(memory_space=pl.ANY)

    def device_step(tokens, w_gate, first_ids, second_ids, keep_two, w_in, w_out):
        seq_len, model_dim = tokens.shape
        num_experts = w_gate.shape[1]
        local_experts, _, ff_dim = w_in.shape
        capacity = max(2, (2 * seq_len + num_experts - 1) // num_experts)
        slab = (local_experts, n, capacity, model_dim)
        lanes = (seq_len // 128, 128)
        return pl.pallas_call(
            functools.partial(layer_kernel, n, local_experts, capacity),
            out_shape=jax.ShapeDtypeStruct((seq_len, model_dim), BF16),
            in_specs=[hbm, vmem, vmem, vmem, vmem, hbm, hbm],
            out_specs=vmem,
            scratch_shapes=[
                pltpu.VMEM((seq_len, model_dim), BF16),
                pltpu.VMEM(slab, BF16),
                pltpu.VMEM(slab, BF16),
                pltpu.VMEM(slab, BF16),
                pltpu.VMEM((2, model_dim, ff_dim), BF16),
                pltpu.VMEM((2, ff_dim, model_dim), BF16),
                pltpu.VMEM((n * capacity, ff_dim), BF16),
                pltpu.VMEM((seq_len, model_dim), F32),
                pltpu.VMEM((seq_len, 128), F32),
                pltpu.SemaphoreType.DMA,
                pltpu.SemaphoreType.DMA((local_experts,)),
                pltpu.SemaphoreType.DMA((local_experts,)),
                pltpu.SemaphoreType.DMA((2, 2)),
                pltpu.SemaphoreType.DMA,
            ],
            compiler_params=pltpu.CompilerParams(collective_id=0, has_side_effects=True, vmem_limit_bytes=VMEM_LIMIT),
        )(
            tokens, w_gate, first_ids.reshape(lanes), second_ids.reshape(lanes), keep_two.reshape(lanes), w_in, w_out
        )

    return jax.shard_map(
        device_step,
        mesh=mesh,
        in_specs=(P(("dp", "ep"), None), P(), token_spec, token_spec, token_spec, P("ep"), P("ep")),
        out_specs=P(("dp", "ep"), None),
        check_vma=False,
    )
```

time: 166 us -> 134 us (0.81)
  Pallas kernels: 161 us -> 131 us
    pallas_call x3 -> x1, Pallas kernels: 161 us -> 131 us  [device_step(): pl.pallas_call(functools.partial(layer_kernel, n, local_experts, capacity...]
    broadcast_in_dim x3 -> x0, local copies, waits for them, and re-layouts: 3.88 us -> none  [the longest x1 1.3 us: device_step(): keep_two[None]]
    unnamed x0 -> x1, local copies, waits for them, and re-layouts: none -> 3.22 us
where the time goes in v2:
time: 134 us
  Pallas kernels  131 us (98%)
  local copies, waits for them, and re-layouts  3.22 us (2%)
    pallas_call x1, Pallas kernels, device_step(): pl.pallas_call(functools.partial(layer_kernel, n, local_experts, capacity...  131 us
    unnamed x1, local copies, waits for them, and re-layouts  3.22 us

profile of v2, /device:TPU:97, one launch (start us, length us, event | category | flops | bytes accessed | tf_op | source)
XLA Modules:
  0.0 134.2 jit_solution(14669395476636106367)
XLA Ops:
  0.0 131.0 %shard_map.73 = bf16[1536,768]{1,0:T(8,128)(2,1)} custom-call(bf16[1536,768]{1,0:T(8,128)(2,1)} %tokens_hbm.1, f32[768,128]{1,0:T(8,128)} %w_gate_ref.1, s32[12,128]{1,0:T(8,128)} %bitcast.3, s32[12,128]{1,0:T(8,128)} %bitcast.4, s32[12,128]{1,0:T(8,128)} %bitcast.5, bf16[4,768,3072]{2,1,0:T(8,128)(2,1)} %w_in_ref.1, bf16[4,3072,768]{2,1,0:T(8,128)(2,1)} %w_out_ref.1), custom_call_target="tpu_custom_call" | custom-call | tf_op jit(solution)/shard_map/pallas_call | solution.py:240
  131.0 3.2 %copy.9 = bf16[1536,768]{1,0:T(8,128)(2,1)} copy(bf16[1536,768]{1,0:T(8,128)(2,1)} %shard_map.73) | data formatting | bytes 4718592
